TPU v7x, 128 devices: a whole 4x4x4 slice. The times are simulated.
128 devices in a mesh: lat: 16 (over z_lo, y, core), lon: 8 (over z_hi, x).
Axes of the slice: x: 4, y: 4, z: 4 (z_hi: 2, z_lo: 2; z = z_hi * 2 + z_lo), core: 2. Of those that a mesh axis runs over, the one named last changes fastest.
Arguments:
- tokens: bfloat16 [4, 128, 256, 1024], P(None, 'lat', 'lon'), may hold values from -6 to 6
- qkv_weight: bfloat16 [3072, 1024], P(('lat', 'lon')), may hold values from -0.1875 to 0.1875
- proj_weight: bfloat16 [1024, 1024], P(('lat', 'lon')), may hold values from -0.1875 to 0.1875
- up_weight: bfloat16 [4096, 1024], P(('lat', 'lon')), may hold values from -0.1875 to 0.1875
- down_weight: bfloat16 [4096, 1024], P(('lat', 'lon')), may hold values from -0.09375 to 0.09375
- bias_table: float32 [225, 16], replicated, may hold values from -3 to 220
- sea_mask: int32 [128, 256], replicated, may hold values 0 or 1
Outputs:
- block_out: bfloat16 [4, 128, 256, 1024], P(None, 'lat', 'lon')
All inputs are finite; a program needn't handle non-finite values.
Results may differ from a plain program's by a relative error of at most 0.012.
Values may be sent and summed in bfloat16 or wider, within the bound.
No kernel may reach another device: no remote copies, remote signals or barrier semaphores. Data moves between devices by JAX's collectives and lax.ppermute only.
A program may use at most 128 MiB of HBM per device.

v0:
```python
import jax
import jax.numpy as jnp
from jax import lax
from jax.sharding import PartitionSpec as P


def from_behind(value, axis, steps):
    count = lax.axis_size(axis)
    pairs = [(source, (source + steps) % count) for source in range(count)]
    return lax.ppermute(value, axis, pairs)


def sent_together(arrays, axis, dim, along):
    ends, at = ([], 0)
    for a in arrays[:-1]:
        at += a.shape[along]
        ends.append(at)
    both = jnp.concatenate(arrays, axis=along)
    return tuple(jnp.split(lax.all_gather(both, axis, axis=dim, tiled=True), ends, axis=along))


def layer_norm(values):
    widened = values.astype(jnp.float32)
    centre = jnp.mean(widened, axis=-1, keepdims=True)
    spread = jnp.mean(jnp.square(widened - centre), axis=-1, keepdims=True)
    return ((widened - centre) * lax.rsqrt(spread + 1e-05)).astype(jnp.bfloat16)


def offsets_table():
    cell_ids = jnp.arange(64, dtype=jnp.int32)
    row_of = cell_ids // 8
    col_of = cell_ids % 8
    return (row_of[:, None] - row_of[None, :] + 7) * 15 + (col_of[:, None] - col_of[None, :] + 7)


def row_region(row_ids, total_rows):
    return jnp.where(row_ids < 4, 2, jnp.where(row_ids >= total_rows - 4, 1, 0)).astype(jnp.int32)


def window_attention(queries, pair_cells, row_start, col_start, sea_mask, pos_bias):
    batch_size, row_count, col_count, feat_width = queries.shape
    head_count = pos_bias.shape[0]
    head_size = feat_width // head_count
    lat_cells, lon_cells = sea_mask.shape
    down_count = row_count // 8
    across_count = col_count // 8
    window_count = down_count * across_count

    def to_windows(values):
        last_dim = values.shape[-1]
        shaped = values.reshape(batch_size, down_count, 8, across_count, 8, last_dim)
        return shaped.transpose(0, 1, 3, 2, 4, 5).reshape(batch_size, window_count, 64, last_dim)

    query_win = to_windows(queries)
    pair_win = to_windows(pair_cells)
    grid_rows = (row_start + jnp.arange(row_count, dtype=jnp.int32)) % lat_cells
    region = row_region(grid_rows, lat_cells).reshape(down_count, 8)
    region = jnp.broadcast_to(region[:, None, :, None], (down_count, across_count, 8, 8)).reshape(
        window_count, 64
    )
    sea_tiled = jnp.tile(sea_mask, (2, 2))
    sea_keep = lax.dynamic_slice(
        sea_tiled, (row_start % lat_cells, col_start % lon_cells), (row_count, col_count)
    )
    sea_keep = (
        sea_keep.reshape(down_count, 8, across_count, 8)
        .transpose(0, 2, 1, 3)
        .reshape(window_count, 64)
        == 1
    )
    same_cell = jnp.eye(64, dtype=bool)
    allowed = (region[:, :, None] == region[:, None, :]) & (sea_keep[:, None, :] | same_cell[None])
    group_width = 4 * head_size
    score_scale = head_size ** (-0.5)

    def one_group(group_index):
        first_col = group_index * group_width
        split_shape = (batch_size, window_count, 64, 4, head_size)
        query_part = lax.dynamic_slice_in_dim(query_win, first_col, group_width, 3).reshape(
            split_shape
        )
        key_part = lax.dynamic_slice_in_dim(pair_win, first_col, group_width, 3).reshape(
            split_shape
        )
        value_part = lax.dynamic_slice_in_dim(
            pair_win, feat_width + first_col, group_width, 3
        ).reshape(split_shape)
        bias_part = lax.dynamic_slice_in_dim(pos_bias, group_index * 4, 4, 0)
        scores = jnp.einsum(
            "bsqhd,bskhd->bshqk", query_part, key_part, preferred_element_type=jnp.float32
        )
        scores = scores * score_scale + bias_part[None, None]
        scores = jnp.where(allowed[None, :, None], scores, -1e30)
        row_top = jnp.max(scores, axis=-1, keepdims=True)
        weights = jnp.exp(scores - row_top)
        attn_probs = (weights / jnp.sum(weights, axis=-1, keepdims=True)).astype(jnp.bfloat16)
        context = jnp.einsum(
            "bshqk,bskhd->bsqhd", attn_probs, value_part, preferred_element_type=jnp.float32
        )
        return context.astype(jnp.bfloat16).reshape(batch_size, window_count, 64, group_width)

    groups = lax.map(one_group, jnp.arange(head_count // 4, dtype=jnp.int32))
    context = jnp.transpose(groups, (1, 2, 3, 0, 4)).reshape(
        batch_size, down_count, across_count, 8, 8, feat_width
    )
    return context.transpose(0, 1, 3, 2, 4, 5).reshape(batch_size, row_count, col_count, feat_width)


def per_device(tokens, qkv_weight, proj_weight, up_weight, down_weight, bias_table, sea_mask):
    batch_size, lat_rows, lon_cols, feat_width = tokens.shape
    head_count = bias_table.shape[1]
    row_base = lax.axis_index("lat") * lat_rows
    col_base = lax.axis_index("lon") * lon_cols
    offset_ids = offsets_table().reshape(-1)
    one_hot = (
        offset_ids[:, None] == jnp.arange(bias_table.shape[0], dtype=jnp.int32)[None, :]
    ).astype(jnp.float32)
    pos_bias = jnp.dot(one_hot, bias_table, precision=lax.Precision.HIGHEST)
    pos_bias = pos_bias.reshape(64, 64, head_count).transpose(2, 0, 1)
    normed = layer_norm(tokens)
    arrived = from_behind(normed[:, :4], "lat", -1)
    rolled_rows = jnp.concatenate([normed[:, 4:], arrived], axis=1)
    arrived_cols = from_behind(rolled_rows[:, :, :4], "lon", -1)
    feed_cells = jnp.concatenate([rolled_rows[:, :, 4:], arrived_cols], axis=2)
    feed_flat = feed_cells.reshape(-1, feat_width)
    projected = lax.dot_general(
        feed_flat,
        lax.all_gather(qkv_weight, ("lat", "lon"), axis=0, tiled=True),
        (((1,), (1,)), ((), ())),
        preferred_element_type=jnp.float32,
    ).astype(jnp.bfloat16)
    projected = projected.reshape(batch_size, lat_rows, lon_cols, 3 * feat_width)
    queries = projected[..., :feat_width]
    pair_cells = projected[..., feat_width:]
    rolled_context = window_attention(
        queries, pair_cells, row_base + 4, col_base + 4, sea_mask, pos_bias
    )
    came_cols = from_behind(rolled_context[:, :, lon_cols - 4 :], "lon", 1)
    back_cols = jnp.concatenate([came_cols, rolled_context[:, :, : lon_cols - 4]], axis=2)
    came_rows = from_behind(back_cols[:, lat_rows - 4 :], "lat", 1)
    context = jnp.concatenate([came_rows, back_cols[:, : lat_rows - 4]], axis=1)
    context_flat = context.reshape(-1, feat_width)
    attention_out = lax.dot_general(
        context_flat,
        lax.all_gather(proj_weight, ("lat", "lon"), axis=0, tiled=True),
        (((1,), (1,)), ((), ())),
        preferred_element_type=jnp.float32,
    )
    attended = (tokens.reshape(-1, feat_width).astype(jnp.float32) + attention_out).astype(
        jnp.bfloat16
    )
    normed_two = layer_norm(attended)
    up_part, down_part = sent_together((up_weight, down_weight), ("lat", "lon"), 0, 1)
    hidden = lax.dot_general(
        normed_two, up_part, (((1,), (1,)), ((), ())), preferred_element_type=jnp.float32
    )
    hidden = jax.nn.gelu(hidden).astype(jnp.bfloat16)
    hidden_sum = jnp.dot(hidden, down_part, preferred_element_type=jnp.float32)
    result = (attended.astype(jnp.float32) + hidden_sum).astype(jnp.bfloat16)
    return result.reshape(tokens.shape)


def solution(mesh):
    placed = (
        P(None, "lat", "lon", None),
        P(("lat", "lon"), None),
        P(("lat", "lon"), None),
        P(("lat", "lon"), None),
        P(("lat", "lon"), None),
        P(),
        P(),
    )
    return jax.shard_map(
        per_device,
        mesh=mesh,
        in_specs=placed,
        out_specs=P(None, "lat", "lon", None),
        check_vma=False,
    )
```

profile of v0, /device:TPU:1, one launch (start us, length us, event | category | flops | bytes accessed | tf_op | source)
XLA Modules:
  0.0 980.6 jit_solution(1794347280123285395)
XLA Ops:
  11.6 2.3 multiply_reduce_fusion
  17.8 2.6 fusion.48
  21.7 9.3 collective-permute-done
  31.1 7.6 collective-permute-start.1
  39.3 4.4 collective-permute-done.1
  44.1 274.7 %all-gather.4.cloned.1.call-done = bf16[3072,1024]{1,0:T(8,128)(2,1)} async-done(((bf16[24,1024]{1,0:T(8,128)(2,1)}), bf16[3072,1024]{1,0:T(8,128)(2,1)}) %all-gather.4.cloned.1.call-update) | async-done | bytes 6291472 | tf_op jit(solution)/shard_map/all_gather | solution.py:128
  318.8 9.7 convolution_convert_fusion.1
  330.0 2.3 copy_bitcast_fusion
  332.4 45.6 %while.13 = (s32[]{:T(128)}, bf16[4,4,4,64,256]{3,4,2,1,0:T(8,128)(2,1)}, s32[4]{0:T(128)S(1)}, bf16[4,4,64,2048]{3,2,1,0:T(8,128)(2,1)}, bf16[4,4,64,1024]{3,2,...) while((s32[]{:T(128)}, ...), condition=%wide.region_5.6_spmd.clone, body=%wide.region_2.5_spmd.clone.sunk | while | flops 69255248 | bytes 12326224 | solution.py:102
  337.6 2.6 fusion.94
  340.7 2.0 convolution_convert_fusion.3
  349.0 2.6 fusion.94
  352.1 2.0 convolution_convert_fusion.3
  360.4 2.6 fusion.94
  363.5 2.0 convolution_convert_fusion.3
  371.8 2.6 fusion.94
  378.0 5.5 copy.28
  383.5 2.7 reshape.220
  389.1 10.5 %collective-permute-done.2 = bf16[4,8,4,1024]{3,2,1,0:T(4,128)(2,1)S(1)} collective-permute-done((bf16[4,8,4,1024]{3,2,1,0:T(4,128)(2,1)S(1)}, bf16[4,8,4,1024]{3,2,1,0:T(4,128)(2,1)S(1)}, u32[]{:S(2)}, u32[]{:S(2)}) %collective-permute-start.2) | collective-permute-done | bytes 262176 | tf_op jit(solution)/shard_map/ppermute | solution.py:10
  401.5 11.7 %collective-permute-done.3 = bf16[4,4,32,1024]{3,2,1,0:T(8,128)(2,1)S(1)} collective-permute-done((bf16[4,4,32,1024]{3,2,1,0:T(8,128)(2,1)S(1)}, bf16[4,4,32,1024]{3,2,1,0:T(8,128)(2,1)S(1)}, u32[]{:S(2)}, u32[]{:S(2)}) %collective-permute-start.3) | collective-permute-done | bytes 1048608 | tf_op jit(solution)/shard_map/ppermute | solution.py:10
  415.1 211.3 %all-gather.6.cloned.1.call-done = bf16[1024,1024]{1,0:T(8,128)(2,1)} async-done(((bf16[8,1024]{1,0:T(8,128)(2,1)}), bf16[1024,1024]{1,0:T(8,128)(2,1)}) %all-gather.6.cloned.1.call-update) | async-done | bytes 2097168 | tf_op jit(solution)/shard_map/all_gather | solution.py:145
  626.3 4.7 convert_reduce_fusion
  633.1 314.2 %all-gather.8.cloned.1.call-done = bf16[4096,2048]{1,0:T(8,128)(2,1)} async-done(((bf16[32,2048]{1,0:T(8,128)(2,1)}), bf16[4096,2048]{1,0:T(8,128)(2,1)}) %all-gather.8.cloned.1.call-update) | async-done | bytes 16777232 | tf_op jit(solution)/shard_map/all_gather | solution.py:19
  947.3 26.8 %fusion.46 = bf16[1024,1024]{1,0:T(8,128)(2,1)} fusion(bf16[1024,1024]{1,0:T(8,128)(2,1)} %copy-done.4, bf16[4096,2048]{1,0:T(8,128)(2,1)} %all-gather.8.cloned.1.call-done, f32[1024]{0:T(1024)S(1)} %add_rsqrt_fusion.1, f32[1024]{0:T(1024)S(1)} %broadcast_multiply_fusion.1), kind=kOutput, calls=%fused_computation.47 | convolution fusion | flops 17224957952 | bytes 23076864 | tf_op jit(solution)/shard_map/dot_general | solution.py:158
  (88 shorter events, 45.2 us)
Async XLA Ops:
  6.5 11.3 %copy-start = (f32[225,16]{0,1:T(8,128)S(1)}, f32[225,16]{0,1:T(8,128)}, u32[]{:S(2)}) copy-start(f32[225,16]{0,1:T(8,128)} %param.14) | copy-start | bytes 43204
  6.5 7.3 copy-start.2
  6.5 312.3 %all-gather.4.cloned.1.call-start = ((), (), s32[]{:S(2)}) async-start(), calls=%async_computation | async-start | bytes 6340608 | tf_op jit(solution)/shard_map/all_gather | solution.py:128
  7.3 619.1 %all-gather.6.cloned.1.call-start = ((), (), s32[]{:S(2)}) async-start(), calls=%async_computation.1 | async-start | bytes 2113536 | tf_op jit(solution)/shard_map/all_gather | solution.py:145
  8.0 939.3 %all-gather.8.cloned.1.call-start = ((), (), s32[]{:S(2)}) async-start(), calls=%async_computation.2 | async-start | bytes 16908288 | tf_op jit(solution)/shard_map/all_gather | solution.py:19
  13.9 3.1 copy-start.5
  15.6 15.4 %collective-permute-start = (bf16[4,4,32,1024]{3,2,1,0:T(8,128)(2,1)}, bf16[4,4,32,1024]{3,2,1,0:T(8,128)(2,1)S(1)}, u32[]{:S(2)}, u32[]{:S(2)}) collective-permute-start(bf16[4,4,32,1024]{3,2,1,0:T(8,128)(2,1)} %get-tuple-element.142), channel_id=1, source_target_pairs={{0,120},{8,0},{16,8},{24,16},{32,24},{40,32},{48,40},{56,48},{64,5... | collective-permute-start | bytes 3145736 | tf_op jit(solution)/shard_map/ppermute | solution.py:10
  31.1 12.6 %collective-permute-start.1 = (bf16[4,8,4,1024]{3,2,1,0:T(4,128)(2,1)S(1)}, bf16[4,8,4,1024]{3,2,1,0:T(4,128)(2,1)S(1)}, u32[]{:S(2)}, u32[]{:S(2)}) collective-permute-start(bf16[4,8,4,1024]{3,2,1,0:T(4,128)(2,1)S(1)} %pad_maximum_fusion.2), channel_id=1, source_target_pairs={{0,7},{1,0},{2,1},{3,2},{4,3},{5,4},{6,5},{7,6},{8,15},{9,8},{10,9... | collective-permute-start | bytes 786440 | tf_op jit(solution)/shard_map/ppermute | solution.py:10
  388.2 11.4 %collective-permute-start.2 = (bf16[4,8,4,1024]{3,2,1,0:T(4,128)(2,1)S(1)}, bf16[4,8,4,1024]{3,2,1,0:T(4,128)(2,1)S(1)}, u32[]{:S(2)}, u32[]{:S(2)}) collective-permute-start(bf16[4,8,4,1024]{3,2,1,0:T(4,128)(2,1)S(1)} %slice.46), channel_id=1, source_target_pairs={{0,1},{1,2},{2,3},{3,4},{4,5},{5,6},{6,7},{7,0},{8,9},{9,10},{10,1... | collective-permute-start | bytes 786440 | tf_op jit(solution)/shard_map/ppermute | solution.py:10
  399.6 226.7 %copy-start.3 = (bf16[4,8,32,1024]{3,2,1,0:T(8,128)(2,1)S(1)}, bf16[4,8,32,1024]{3,2,1,0:T(8,128)(2,1)}, u32[]{:S(2)}) copy-start(bf16[4,8,32,1024]{3,2,1,0:T(8,128)(2,1)} %param.9) | copy-start | bytes 6291460
  400.0 13.2 %collective-permute-start.3 = (bf16[4,4,32,1024]{3,2,1,0:T(8,128)(2,1)S(1)}, bf16[4,4,32,1024]{3,2,1,0:T(8,128)(2,1)S(1)}, u32[]{:S(2)}, u32[]{:S(2)}) collective-permute-start(bf16[4,4,32,1024]{3,2,1,0:T(8,128)(2,1)S(1)} %fusion.68), channel_id=1, source_target_pairs={{0,8},{8,16},{16,24},{24,32},{32,40},{40,48},{48,56},{56,64},{64,7... | collective-permute-start | bytes 3145736 | tf_op jit(solution)/shard_map/ppermute | solution.py:10
  631.0 1.4 copy-start.4
  947.3 26.8 %copy-start.1 = (f32[225,16]{0,1:T(8,128)S(1)}, f32[225,16]{0,1:T(8,128)}, u32[]{:S(2)}) copy-start(f32[225,16]{0,1:T(8,128)} %param.14) | copy-start | bytes 43204
Sparse Core Ops, SparseCore 0:
  9.0 309.7 all-gather.3
  320.5 305.8 all-gather.5
  628.0 319.1 all-gather.7
where the time goes:
time: 981 us
  waiting for transfers between devices  838 us (85%)
  matrix products  62.2 us (6%)
  local copies, waits for them, and re-layouts  39.9 us (4%)
  between operations  13.3 us (1%)
  starting transfers between devices  11.5 us (1%)
  other arithmetic  10.9 us (1%)
    all_gather x1, waiting for transfers between devices, sent_together(): lax.all_gather(both, axis, axis=dim, tiled=True)  314 us
    all_gather x1, waiting for transfers between devices, per_device(): lax.all_gather(qkv_weight, ('lat', 'lon'), axis=0, tiled=True)  275 us
    all_gather x1, waiting for transfers between devices, per_device(): lax.all_gather(proj_weight, ('lat', 'lon'), axis=0, tiled=True)  211 us
    ppermute x4, waiting for transfers between devices, from_behind(): return lax.ppermute(value, axis, pairs)  36 us
    dot_general x1, matrix products, per_device(): hidden_sum = jnp.dot(hidden, down_part, preferred_element_type=jnp.float32)  26.8 us
  transfers between devices with their start and end apart: 7, of which 7 were waited for; matrix products, arithmetic and copies ran while one was open for 9% of the time, Pallas kernels for 0%

commit v1 on v0

--- a/solution.py
+++ b/solution.py
@@ -1,22 +1,38 @@
+import math
+
 import jax
 import jax.numpy as jnp
 from jax import lax
+from jax.sharding import Mesh
 from jax.sharding import PartitionSpec as P
 
 
 def from_behind(value, axis, steps):
-    count = lax.axis_size(axis)
+    count = math.prod(lax.axis_size(a) for a in axis)
     pairs = [(source, (source + steps) % count) for source in range(count)]
     return lax.ppermute(value, axis, pairs)
 
 
-def sent_together(arrays, axis, dim, along):
-    ends, at = ([], 0)
-    for a in arrays[:-1]:
-        at += a.shape[along]
-        ends.append(at)
-    both = jnp.concatenate(arrays, axis=along)
-    return tuple(jnp.split(lax.all_gather(both, axis, axis=dim, tiled=True), ends, axis=along))
+AXES = ("zl", "y", "c", "zh", "x")
+SIZES = (2, 4, 2, 2, 4)
+LAT = ("zl", "y", "c")
+LON = ("zh", "x")
+TORUS = ("zh", "zl", "y", "x", "c")
+TO_LOGICAL = tuple(TORUS.index(a) for a in AXES)
+
+
+def gather_weights(arrays):
+    rows = [a.shape[0] for a in arrays]
+    width = arrays[0].shape[1]
+    both = jnp.concatenate(arrays, axis=0)
+    every = lax.all_gather(both, TORUS, axis=0, tiled=True)
+    every = every.reshape(tuple(SIZES[AXES.index(a)] for a in TORUS) + both.shape)
+    out, at = [], 0
+    for count in rows:
+        part = every[..., at : at + count, :]
+        at += count
+        out.append(part.transpose(TO_LOGICAL + (5, 6)).reshape(-1, width))
+    return out
 
 
 def layer_norm(values):
@@ -109,23 +125,26 @@
 def per_device(tokens, qkv_weight, proj_weight, up_weight, down_weight, bias_table, sea_mask):
     batch_size, lat_rows, lon_cols, feat_width = tokens.shape
     head_count = bias_table.shape[1]
-    row_base = lax.axis_index("lat") * lat_rows
-    col_base = lax.axis_index("lon") * lon_cols
+    row_base = ((lax.axis_index("zl") * 4 + lax.axis_index("y")) * 2 + lax.axis_index("c")) * lat_rows
+    col_base = (lax.axis_index("zh") * 4 + lax.axis_index("x")) * lon_cols
     offset_ids = offsets_table().reshape(-1)
     one_hot = (
         offset_ids[:, None] == jnp.arange(bias_table.shape[0], dtype=jnp.int32)[None, :]
     ).astype(jnp.float32)
     pos_bias = jnp.dot(one_hot, bias_table, precision=lax.Precision.HIGHEST)
     pos_bias = pos_bias.reshape(64, 64, head_count).transpose(2, 0, 1)
+    qkv_all, proj_all, up_part, down_part = gather_weights(
+        (qkv_weight, proj_weight, up_weight, down_weight)
+    )
     normed = layer_norm(tokens)
-    arrived = from_behind(normed[:, :4], "lat", -1)
+    arrived = from_behind(normed[:, :4], LAT, -1)
     rolled_rows = jnp.concatenate([normed[:, 4:], arrived], axis=1)
-    arrived_cols = from_behind(rolled_rows[:, :, :4], "lon", -1)
+    arrived_cols = from_behind(rolled_rows[:, :, :4], LON, -1)
     feed_cells = jnp.concatenate([rolled_rows[:, :, 4:], arrived_cols], axis=2)
     feed_flat = feed_cells.reshape(-1, feat_width)
     projected = lax.dot_general(
         feed_flat,
-        lax.all_gather(qkv_weight, ("lat", "lon"), axis=0, tiled=True),
+        qkv_all,
         (((1,), (1,)), ((), ())),
         preferred_element_type=jnp.float32,
     ).astype(jnp.bfloat16)
@@ -135,14 +154,14 @@
     rolled_context = window_attention(
         queries, pair_cells, row_base + 4, col_base + 4, sea_mask, pos_bias
     )
-    came_cols = from_behind(rolled_context[:, :, lon_cols - 4 :], "lon", 1)
+    came_cols = from_behind(rolled_context[:, :, lon_cols - 4 :], LON, 1)
     back_cols = jnp.concatenate([came_cols, rolled_context[:, :, : lon_cols - 4]], axis=2)
-    came_rows = from_behind(back_cols[:, lat_rows - 4 :], "lat", 1)
+    came_rows = from_behind(back_cols[:, lat_rows - 4 :], LAT, 1)
     context = jnp.concatenate([came_rows, back_cols[:, : lat_rows - 4]], axis=1)
     context_flat = context.reshape(-1, feat_width)
     attention_out = lax.dot_general(
         context_flat,
-        lax.all_gather(proj_weight, ("lat", "lon"), axis=0, tiled=True),
+        proj_all,
         (((1,), (1,)), ((), ())),
         preferred_element_type=jnp.float32,
     )
@@ -150,7 +169,6 @@
         jnp.bfloat16
     )
     normed_two = layer_norm(attended)
-    up_part, down_part = sent_together((up_weight, down_weight), ("lat", "lon"), 0, 1)
     hidden = lax.dot_general(
         normed_two, up_part, (((1,), (1,)), ((), ())), preferred_element_type=jnp.float32
     )
@@ -161,19 +179,12 @@
 
 
 def solution(mesh):
-    placed = (
-        P(None, "lat", "lon", None),
-        P(("lat", "lon"), None),
-        P(("lat", "lon"), None),
-        P(("lat", "lon"), None),
-        P(("lat", "lon"), None),
-        P(),
-        P(),
-    )
+    torus = Mesh(mesh.devices.reshape(SIZES), AXES)
+    rows = P(LAT + LON, None)
     return jax.shard_map(
         per_device,
-        mesh=mesh,
-        in_specs=placed,
-        out_specs=P(None, "lat", "lon", None),
+        mesh=torus,
+        in_specs=(P(None, LAT, LON, None), rows, rows, rows, rows, P(), P()),
+        out_specs=P(None, LAT, LON, None),
         check_vma=False,
     )

time: 981 us -> 271 us (0.28)
  waiting for transfers between devices: 838 us -> 91.5 us
  local copies, waits for them, and re-layouts: 39.9 us -> 76.1 us
    all_gather x3 -> x1, waiting for transfers between devices: 800 us -> 71.3 us  [gather_weights(): every = lax.all_gather(both, TORUS, axis=0, tiled=True)]
    transpose x0 -> x7, local copies, waits for them, and re-layouts: none -> 35.8 us  [gather_weights(): out.append(part.transpose(TO_LOGICAL + (5, 6)).reshape(-1, width))]
    ppermute x4, waiting for transfers between devices: 36 us -> 20.1 us  [from_behind(): return lax.ppermute(value, axis, pairs)]
  transfers between devices with their start and end apart: 7 -> 5, of which waited for: 7 -> 4; matrix products, arithmetic and copies ran while one was open for 9% -> 16% of each run, Pallas kernels for 0% -> 0%
where the time goes in v1:
time: 271 us; the launch traced here: 270 us
  waiting for transfers between devices  91.5 us (34%)
  local copies, waits for them, and re-layouts  76.1 us (28%)
  matrix products  61.5 us (23%)
  between operations  13.6 us (5%)
  starting transfers between devices  12.3 us (5%)
  other arithmetic  10.4 us (4%)
  loops' own time  4.81 us (2%)
    all_gather x1, waiting for transfers between devices, gather_weights(): every = lax.all_gather(both, TORUS, axis=0, tiled=True)  71.3 us
    transpose x7, local copies, waits for them, and re-layouts, gather_weights(): out.append(part.transpose(TO_LOGICAL + (5, 6)).reshape(-1, width))  35.8 us
    dot_general x1, matrix products, per_device(): hidden_sum = jnp.dot(hidden, down_part, preferred_element_type=jnp.float32)  25.8 us
    ppermute x4, waiting for transfers between devices, from_behind(): return lax.ppermute(value, axis, pairs)  20.1 us
    sub x4, matrix products, one_group(): weights = jnp.exp(scores - row_top)  15.2 us
    ppermute x4, starting transfers between devices, from_behind(): return lax.ppermute(value, axis, pairs)  12.3 us
    dot_general x4, matrix products, one_group(): jnp.einsum('bshqk,bskhd->bsqhd', attn_probs, value_part, preferred_elemen...  8.3 us
    dot_general x1, matrix products, per_device(): lax.dot_general(feed_flat, qkv_all, (((1,), (1,)), ((), ())), preferred_e...  7.19 us
  transfers between devices with their start and end apart: 5, of which 4 were waited for; matrix products, arithmetic and copies ran while one was open for 16% of the time, Pallas kernels for 0%

profile of v1, /device:TPU:1, one launch (start us, length us, event | category | flops | bytes accessed | tf_op | source)
XLA Modules:
  0.0 270.2 jit_solution(7870842900243886426)
XLA Ops:
  10.2 2.3 multiply_reduce_fusion
  15.9 2.6 fusion.42
  21.0 9.3 %collective-permute-done = bf16[4,4,32,1024]{3,2,1,0:T(8,128)(2,1)S(1)} collective-permute-done((bf16[4,4,32,1024]{3,2,1,0:T(8,128)(2,1)}, bf16[4,4,32,1024]{3,2,1,0:T(8,128)(2,1)S(1)}, u32[]{:S(2)}, u32[]{:S(2)}) %collective-permute-start) | collective-permute-done | bytes 1048608 | tf_op jit(solution)/shard_map/ppermute | solution.py:13
  30.5 7.1 %collective-permute-start.1 = (bf16[4,8,4,1024]{3,2,1,0:T(4,128)(2,1)S(1)}, bf16[4,8,4,1024]{3,2,1,0:T(4,128)(2,1)S(1)}, u32[]{:S(2)}, u32[]{:S(2)}) collective-permute-start(bf16[4,8,4,1024]{3,2,1,0:T(4,128)(2,1)S(1)} %pad_maximum_fusion.2), channel_id=1, source_target_pairs={{0,7},{1,0},{2,1},{3,2},{4,3},{5,4},{6,5},{7,6},{8,15},{9,8},{10,9... | collective-permute-start | bytes 786440 | tf_op jit(solution)/shard_map/ppermute | solution.py:13
  38.2 2.8 %collective-permute-done.1 = bf16[4,8,4,1024]{3,2,1,0:T(4,128)(2,1)S(1)} collective-permute-done((bf16[4,8,4,1024]{3,2,1,0:T(4,128)(2,1)S(1)}, bf16[4,8,4,1024]{3,2,1,0:T(4,128)(2,1)S(1)}, u32[]{:S(2)}, u32[]{:S(2)}) %collective-permute-start.1) | collective-permute-done | bytes 262176 | tf_op jit(solution)/shard_map/ppermute | solution.py:13
  41.3 71.3 %all-gather.2.cloned.1.call-done = bf16[12288,1024]{1,0:T(8,128)(2,1)} async-done(((bf16[96,1024]{1,0:T(8,128)(2,1)}), bf16[12288,1024]{1,0:T(8,128)(2,1)}) %all-gather.2.cloned.1.call-update) | async-done | bytes 25165840 | tf_op jit(solution)/shard_map/all_gather | solution.py:28
  112.7 3.5 %slice_bitcast_fusion.2 = bf16[2,4,2,2,4,24,1024]{6,5,2,4,1,0,3:T(8,128)(2,1)S(1)} fusion(bf16[2,2,4,4,2,96,1024]{6,5,4,3,2,1,0:T(8,128)(2,1)} %bitcast.81), kind=kLoop, calls=%fused_computation.35 | loop fusion | bytes 12582912 | tf_op jit(solution)/shard_map/transpose | solution.py:34
  117.2 7.2 %convolution_convert_fusion.1 = bf16[1024,3072]{1,0:T(8,128)(2,1)S(1)} fusion(bf16[1024,1024]{1,0:T(8,128)(2,1)S(1)} %bitcast.95, bf16[3072,1024]{1,0:T(8,128)(2,1)S(1)} %bitcast.88), kind=kOutput, calls=%fused_computation.39 | convolution fusion | flops 6445596672 | bytes 14680064 | tf_op jit(solution)/shard_map/dot_general | solution.py:145
  124.4 2.3 copy_bitcast_fusion
  128.3 50.9 %while.13 = (s32[]{:T(128)}, bf16[4,4,4,64,256]{3,4,2,1,0:T(8,128)(2,1)}, s32[4]{0:T(128)S(1)}, bf16[4,4,64,2048]{3,2,1,0:T(8,128)(2,1)}, bf16[4,4,64,1024]{3,2,...) while((s32[]{:T(128)}, ...), condition=%wide.region_5.6_spmd.clone, body=%wide.region_2.5_spmd.clone.sunk | while | flops 69255248 | bytes 14422932 | solution.py:118
  134.0 3.8 %fusion.87 = (f32[4,4,4,64]{3,2,1,0:T(4,128)S(1)}, f32[4,4,4,64,64]{3,4,2,1,0:T(8,128)}) fusion(f32[4,64,64]{1,2,0:T(8,128)S(1)} %constant_dynamic-slice_fusion.7, pred[4,64,64]{1,2,0:T(8,128)(4,1)S(1)} %or_and_fusion.2, bf16[4,4,64,4,64]{4,3,2,1,0:T(4,128)(2,1)S(1)} %reshape.250, bf16[4,4,64,4,64]{4,3,2,1,0:T(4,128)(2,1)} %reshape.251), kind=kOutput, calls=%fused_computation.93.clone.1 | convolution fusion | flops 34865216 | bytes 2195456 | tf_op jit(solution)/shard_map/while/body/eval_jaxpr/sub | solution.py:111
  146.8 3.8 %fusion.87 = (f32[4,4,4,64]{3,2,1,0:T(4,128)S(1)}, f32[4,4,4,64,64]{3,4,2,1,0:T(8,128)}) fusion(f32[4,64,64]{1,2,0:T(8,128)S(1)} %constant_dynamic-slice_fusion.7, pred[4,64,64]{1,2,0:T(8,128)(4,1)S(1)} %or_and_fusion.2, bf16[4,4,64,4,64]{4,3,2,1,0:T(4,128)(2,1)S(1)} %reshape.250, bf16[4,4,64,4,64]{4,3,2,1,0:T(4,128)(2,1)} %reshape.251), kind=kOutput, calls=%fused_computation.93.clone.1 | convolution fusion | flops 34865216 | bytes 2195456 | tf_op jit(solution)/shard_map/while/body/eval_jaxpr/sub | solution.py:111
  159.5 3.8 %fusion.87 = (f32[4,4,4,64]{3,2,1,0:T(4,128)S(1)}, f32[4,4,4,64,64]{3,4,2,1,0:T(8,128)}) fusion(f32[4,64,64]{1,2,0:T(8,128)S(1)} %constant_dynamic-slice_fusion.7, pred[4,64,64]{1,2,0:T(8,128)(4,1)S(1)} %or_and_fusion.2, bf16[4,4,64,4,64]{4,3,2,1,0:T(4,128)(2,1)S(1)} %reshape.250, bf16[4,4,64,4,64]{4,3,2,1,0:T(4,128)(2,1)} %reshape.251), kind=kOutput, calls=%fused_computation.93.clone.1 | convolution fusion | flops 34865216 | bytes 2195456 | tf_op jit(solution)/shard_map/while/body/eval_jaxpr/sub | solution.py:111
  172.2 3.8 %fusion.87 = (f32[4,4,4,64]{3,2,1,0:T(4,128)S(1)}, f32[4,4,4,64,64]{3,4,2,1,0:T(8,128)}) fusion(f32[4,64,64]{1,2,0:T(8,128)S(1)} %constant_dynamic-slice_fusion.7, pred[4,64,64]{1,2,0:T(8,128)(4,1)S(1)} %or_and_fusion.2, bf16[4,4,64,4,64]{4,3,2,1,0:T(4,128)(2,1)S(1)} %reshape.250, bf16[4,4,64,4,64]{4,3,2,1,0:T(4,128)(2,1)} %reshape.251), kind=kOutput, calls=%fused_computation.93.clone.1 | convolution fusion | flops 34865216 | bytes 2195456 | tf_op jit(solution)/shard_map/while/body/eval_jaxpr/sub | solution.py:111
  176.0 2.1 convolution_convert_fusion.3
  179.2 5.5 %copy.29 = bf16[4,4,64,4,256]{4,3,2,1,0:T(4,128)(2,1)S(1)} copy(bf16[4,4,64,4,256]{2,4,1,0,3:T(8,128)(2,1)} %bitcast.91) | data formatting | bytes 4194304 | tf_op jit(solution)/shard_map/transpose | solution.py:119
  184.7 2.7 %reshape.237 = bf16[4,1,4,8,8,1024]{5,4,3,2,0,1:T(8,128)(2,1)} reshape(bf16[4,4,64,4,256]{4,3,2,1,0:T(4,128)(2,1)S(1)} %copy.29) | data formatting | bytes 4194304 | tf_op jit(solution)/shard_map/reshape | solution.py:119
  192.6 8.0 %collective-permute-done.2 = bf16[4,8,4,1024]{3,2,1,0:T(4,128)(2,1)S(1)} collective-permute-done((bf16[4,8,4,1024]{3,2,1,0:T(4,128)(2,1)S(1)}, bf16[4,8,4,1024]{3,2,1,0:T(4,128)(2,1)S(1)}, u32[]{:S(2)}, u32[]{:S(2)}) %collective-permute-start.2) | collective-permute-done | bytes 262176 | tf_op jit(solution)/shard_map/ppermute | solution.py:13
  201.0 2.5 collective-permute-start.3
  203.5 12.3 %slice_bitcast_fusion.1 = (bf16[2,4,2,2,4,32,1024]{6,5,2,4,1,0,3:T(8,128)(2,1)}, bf16[2,4,2,2,4,32,1024]{6,5,2,4,1,0,3:T(8,128)(2,1)}) fusion(bf16[2,2,4,4,2,96,1024]{6,5,4,3,2,1,0:T(8,128)(2,1)} %bitcast.83), kind=kLoop, calls=%fused_computation.33 | loop fusion | bytes 33554432 | tf_op jit(solution)/shard_map/transpose | solution.py:34
  215.8 8.5 %copy.33 = bf16[2,4,2,2,4,32,1024]{6,5,4,3,2,1,0:T(8,128)(2,1)} copy(bf16[2,4,2,2,4,32,1024]{6,5,2,4,1,0,3:T(8,128)(2,1)} %get-tuple-element.142) | data formatting | bytes 16777216 | tf_op jit(solution)/shard_map/transpose | solution.py:34
  224.3 8.5 %copy.32 = bf16[2,4,2,2,4,32,1024]{6,5,4,3,2,1,0:T(8,128)(2,1)} copy(bf16[2,4,2,2,4,32,1024]{6,5,2,4,1,0,3:T(8,128)(2,1)} %get-tuple-element.141) | data formatting | bytes 16777216 | tf_op jit(solution)/shard_map/transpose | solution.py:34
  234.4 2.5 convert_reduce_fusion
  237.5 25.8 %fusion.40 = bf16[1024,1024]{1,0:T(8,128)(2,1)} fusion(bf16[1024,1024]{1,0:T(8,128)(2,1)S(1)} %get-tuple-element.146, bf16[4096,1024]{1,0:T(8,128)(2,1)} %bitcast.86, bf16[4096,1024]{1,0:T(8,128)(2,1)} %bitcast.87, f32[1024]{0:T(1024)S(1)} %add_rsqrt_fusion.1, f32[1024]{0:T(1024)S(1)} %broadcast_multiply_fusion.1), kind=kOutput, calls=%fused_computation.44 | convolution fusion | flops 17224957952 | bytes 20979712 | tf_op jit(solution)/shard_map/dot_general | solution.py:176
  (103 shorter events, 49.8 us)
Async XLA Ops:
  6.5 9.3 %copy-start = (f32[225,16]{0,1:T(8,128)S(1)}, f32[225,16]{0,1:T(8,128)}, u32[]{:S(2)}) copy-start(f32[225,16]{0,1:T(8,128)} %param.14) | copy-start | bytes 43204
  6.5 6.0 %copy-start.2 = (bf16[4,8,32,1024]{3,2,1,0:T(8,128)(2,1)S(1)}, bf16[4,8,32,1024]{3,2,1,0:T(8,128)(2,1)}, u32[]{:S(2)}) copy-start(bf16[4,8,32,1024]{3,2,1,0:T(8,128)(2,1)} %param.9) | copy-start | bytes 6291460
  6.5 106.1 %all-gather.2.cloned.1.call-start = ((), (), s32[]{:S(2)}) async-start(), calls=%async_computation | async-start | bytes 25362432 | tf_op jit(solution)/shard_map/all_gather | solution.py:28
  13.1 5.9 %copy-start.6 = (s32[128,256]{1,0:T(8,128)S(1)}, s32[128,256]{1,0:T(8,128)}, u32[]{:S(2)}) copy-start(s32[128,256]{1,0:T(8,128)} %param.15) | copy-start | bytes 393220
  14.3 16.1 %collective-permute-start = (bf16[4,4,32,1024]{3,2,1,0:T(8,128)(2,1)}, bf16[4,4,32,1024]{3,2,1,0:T(8,128)(2,1)S(1)}, u32[]{:S(2)}, u32[]{:S(2)}) collective-permute-start(bf16[4,4,32,1024]{3,2,1,0:T(8,128)(2,1)} %get-tuple-element.144), channel_id=1, source_target_pairs={{0,120},{8,0},{16,8},{24,16},{32,24},{40,32},{48,40},{56,48},{64,5... | collective-permute-start | bytes 3145736 | tf_op jit(solution)/shard_map/ppermute | solution.py:13
  30.5 10.5 %collective-permute-start.1 = (bf16[4,8,4,1024]{3,2,1,0:T(4,128)(2,1)S(1)}, bf16[4,8,4,1024]{3,2,1,0:T(4,128)(2,1)S(1)}, u32[]{:S(2)}, u32[]{:S(2)}) collective-permute-start(bf16[4,8,4,1024]{3,2,1,0:T(4,128)(2,1)S(1)} %pad_maximum_fusion.2), channel_id=1, source_target_pairs={{0,7},{1,0},{2,1},{3,2},{4,3},{5,4},{6,5},{7,6},{8,15},{9,8},{10,9... | collective-permute-start | bytes 786440 | tf_op jit(solution)/shard_map/ppermute | solution.py:13
  128.3 3.9 %copy-start.4 = (f32[16,64,64]{1,2,0:T(8,128)}, f32[16,64,64]{1,2,0:T(8,128)S(1)}, u32[]{:S(2)}) copy-start(f32[16,64,64]{1,2,0:T(8,128)S(1)} %get-tuple-element.253) | copy-start | bytes 786436 | tf_op jit(solution)/shard_map/while
  137.8 3.2 %copy-start.5 = (f32[16,64,64]{1,2,0:T(8,128)S(1)}, f32[16,64,64]{1,2,0:T(8,128)}, u32[]{:S(2)}) copy-start(f32[16,64,64]{1,2,0:T(8,128)} %copy-done.4) | copy-start | bytes 786436 | tf_op jit(solution)/shard_map/while
  141.0 3.9 %copy-start.4 = (f32[16,64,64]{1,2,0:T(8,128)}, f32[16,64,64]{1,2,0:T(8,128)S(1)}, u32[]{:S(2)}) copy-start(f32[16,64,64]{1,2,0:T(8,128)S(1)} %get-tuple-element.253) | copy-start | bytes 786436 | tf_op jit(solution)/shard_map/while
  150.6 3.1 %copy-start.5 = (f32[16,64,64]{1,2,0:T(8,128)S(1)}, f32[16,64,64]{1,2,0:T(8,128)}, u32[]{:S(2)}) copy-start(f32[16,64,64]{1,2,0:T(8,128)} %copy-done.4) | copy-start | bytes 786436 | tf_op jit(solution)/shard_map/while
  153.7 3.9 %copy-start.4 = (f32[16,64,64]{1,2,0:T(8,128)}, f32[16,64,64]{1,2,0:T(8,128)S(1)}, u32[]{:S(2)}) copy-start(f32[16,64,64]{1,2,0:T(8,128)S(1)} %get-tuple-element.253) | copy-start | bytes 786436 | tf_op jit(solution)/shard_map/while
  163.3 3.2 %copy-start.5 = (f32[16,64,64]{1,2,0:T(8,128)S(1)}, f32[16,64,64]{1,2,0:T(8,128)}, u32[]{:S(2)}) copy-start(f32[16,64,64]{1,2,0:T(8,128)} %copy-done.4) | copy-start | bytes 786436 | tf_op jit(solution)/shard_map/while
  166.5 3.9 %copy-start.4 = (f32[16,64,64]{1,2,0:T(8,128)}, f32[16,64,64]{1,2,0:T(8,128)S(1)}, u32[]{:S(2)}) copy-start(f32[16,64,64]{1,2,0:T(8,128)S(1)} %get-tuple-element.253) | copy-start | bytes 786436 | tf_op jit(solution)/shard_map/while
  176.0 3.2 %copy-start.5 = (f32[16,64,64]{1,2,0:T(8,128)S(1)}, f32[16,64,64]{1,2,0:T(8,128)}, u32[]{:S(2)}) copy-start(f32[16,64,64]{1,2,0:T(8,128)} %copy-done.4) | copy-start | bytes 786436 | tf_op jit(solution)/shard_map/while
  189.3 11.3 %collective-permute-start.2 = (bf16[4,8,4,1024]{3,2,1,0:T(4,128)(2,1)S(1)}, bf16[4,8,4,1024]{3,2,1,0:T(4,128)(2,1)S(1)}, u32[]{:S(2)}, u32[]{:S(2)}) collective-permute-start(bf16[4,8,4,1024]{3,2,1,0:T(4,128)(2,1)S(1)} %slice.63), channel_id=1, source_target_pairs={{0,1},{1,2},{2,3},{3,4},{4,5},{5,6},{6,7},{7,0},{8,9},{9,10},{10,1... | collective-permute-start | bytes 786440 | tf_op jit(solution)/shard_map/ppermute | solution.py:13
  201.0 31.7 %collective-permute-start.3 = (bf16[4,4,32,1024]{3,2,1,0:T(8,128)(2,1)S(1)}, bf16[4,4,32,1024]{3,2,1,0:T(8,128)(2,1)S(1)}, u32[]{:S(2)}, u32[]{:S(2)}) collective-permute-start(bf16[4,4,32,1024]{3,2,1,0:T(8,128)(2,1)S(1)} %fusion.59), channel_id=1, source_target_pairs={{0,8},{8,16},{16,24},{24,32},{32,40},{40,48},{48,56},{56,64},{64,7... | collective-permute-start | bytes 3145736 | tf_op jit(solution)/shard_map/ppermute | solution.py:13
  232.8 1.6 copy-start.3
  237.5 25.8 %copy-start.1 = (f32[225,16]{0,1:T(8,128)S(1)}, f32[225,16]{0,1:T(8,128)}, u32[]{:S(2)}) copy-start(f32[225,16]{0,1:T(8,128)} %param.14) | copy-start | bytes 43204
Sparse Core Ops, SparseCore 0:
  10.4 102.1 all-gather.1

commit v2 on v1

v2 whole, which is shorter than its diff:
```python
import jax
import jax.numpy as jnp
from jax import lax
from jax.experimental import pallas as pl
from jax.experimental.pallas import tpu as pltpu
from jax.sharding import Mesh
from jax.sharding import PartitionSpec as P

BF = jnp.bfloat16
F32 = jnp.float32
NT = (((1,), (1,)), ((), ()))
VMEM_LIMIT = 60 * 1024 * 1024


def block_copies(src, dst, first, count, sem):
    copies = []
    for zl in range(2):
        for y in range(4):
            for c in range(2):
                for zh in range(2):
                    copies.append(
                        pltpu.make_async_copy(
                            src.at[zh, zl, y, :, c, pl.ds(first, count), :],
                            dst.at[zl, y, c, zh],
                            sem,
                        )
                    )
    return copies


def attention_kernel(x_ref, every_ref, bias_ref, mask_ref, out_ref, w_ref, xw_ref, qkv_ref, sem):
    samples = x_ref.shape[0]

    @pl.when(pl.program_id(0) == 0)
    def _():
        for copy in block_copies(every_ref, w_ref, 0, 24, sem):
            copy.start()

    for s in range(samples):
        for w in range(4):
            xw_ref[pl.ds((s * 4 + w) * 64, 64), :] = x_ref[s, :, w].reshape(64, 1024)

    @pl.when(pl.program_id(0) == 0)
    def _():
        pltpu.make_async_copy(w_ref, w_ref, sem).wait()

    weights = w_ref.reshape(3072, 1024)
    for n in range(6):
        y = lax.dot_general(
            xw_ref[...], weights[pl.ds(n * 512, 512), :], NT, preferred_element_type=F32
        )
        if n < 2:
            y = y * 0.125
        qkv_ref[:, pl.ds(n * 512, 512)] = y.astype(BF)

    low = lax.broadcasted_iota(jnp.int32, (128, 128), 1) < 64
    zero = jnp.zeros((128, 128), BF)
    ones = jnp.ones((128, 128), BF)

    @pl.loop(0, samples * 2)
    def _(pair):
        rows = pl.ds(pl.multiple_of(pair * 128, 128), 128)
        sample, half = pair // 2, pair % 2
        mask = mask_ref[half]
        for j in range(8):
            q = qkv_ref[rows, pl.ds(j * 128, 128)]
            k = qkv_ref[rows, pl.ds(1024 + j * 128, 128)]
            v = qkv_ref[rows, pl.ds(2048 + j * 128, 128)]
            both = jnp.concatenate([jnp.where(low, q, zero), jnp.where(low, zero, q)], axis=0)
            scores = lax.dot_general(both, k, NT, preferred_element_type=F32)
            scores = scores.reshape(2, 128, 128) + bias_ref[pl.ds(2 * j, 2)] + mask[None]
            scores = scores.reshape(256, 128)
            top = jnp.max(scores, axis=-1, keepdims=True)
            probs = jnp.exp(scores - top).astype(BF)
            summed = jnp.dot(probs, jnp.concatenate([v, ones], axis=1), preferred_element_type=F32)
            context = summed[:, :128] / summed[:, 128:]
            context = jnp.where(low, context[:128], context[128:]).astype(BF)
            for i in range(2):
                out_ref[sample, :, half * 2 + i, :, pl.ds(j * 128, 128)] = context[
                    i * 64 : (i + 1) * 64
                ].reshape(8, 8, 128)


def attention(feed, every, bias, mask, step=2):
    batch = feed.shape[0]
    width = 1024
    tokens = step * 256
    return pl.pallas_call(
        attention_kernel,
        grid=(batch // step,),
        in_specs=[
            pl.BlockSpec((step, 8, 4, 8, width), lambda i: (i, 0, 0, 0, 0)),
            pl.BlockSpec(memory_space=pl.ANY),
            pl.BlockSpec((16, 128, 128), lambda i: (0, 0, 0)),
            pl.BlockSpec((2, 128, 128), lambda i: (0, 0, 0)),
        ],
        out_specs=pl.BlockSpec((step, 8, 4, 8, width), lambda i: (i, 0, 0, 0, 0)),
        out_shape=jax.ShapeDtypeStruct((batch, 8, 4, 8, width), BF),
        scratch_shapes=[
            pltpu.VMEM((2, 4, 2, 2, 4, 24, width), BF),
            pltpu.VMEM((tokens, width), BF),
            pltpu.VMEM((tokens, 3 * width), BF),
            pltpu.SemaphoreType.DMA,
        ],
        compiler_params=pltpu.CompilerParams(
            dimension_semantics=("arbitrary",), vmem_limit_bytes=VMEM_LIMIT
        ),
        cost_estimate=pl.CostEstimate(
            flops=2 * batch * 256 * width * 3 * width,
            bytes_accessed=12 << 20,
            transcendentals=batch * 256 * 1024,
        ),
        name="attention",
    )(feed, every, bias, mask)


def normed_rows(values):
    wide = values.astype(F32)
    centre = jnp.mean(wide, axis=-1, keepdims=True)
    shifted = wide - centre
    spread = jnp.mean(shifted * shifted, axis=-1, keepdims=True)
    return (shifted * lax.rsqrt(spread + 1e-05)).astype(BF)


def gelu(x):
    inner = x * (0.7978845608028654 + 0.035677408136300125 * (x * x))
    half = 0.5 * x
    return half + half * jnp.tanh(inner)


def tail_kernel(ctx_ref, tok_ref, every_ref, up_ref, down_ref, out_ref, w_ref, n_ref, acc_ref, sem):
    step = pl.program_id(0)
    rows = ctx_ref.shape[0]
    tile = 256

    @pl.when(step == 0)
    def _():
        for copy in block_copies(every_ref, w_ref, 24, 8, sem):
            copy.start()
        pltpu.make_async_copy(w_ref, w_ref, sem).wait()
        for m in range(rows // tile):
            at = pl.ds(m * tile, tile)
            out = lax.dot_general(
                ctx_ref[at, :], w_ref.reshape(1024, 1024)[...], NT, preferred_element_type=F32
            )
            attended = (tok_ref[at, :].astype(F32) + out).astype(BF)
            acc_ref[at, :] = attended.astype(F32)
            n_ref[at, :] = normed_rows(attended)

    up = up_ref[...].reshape(-1, 1024)
    down = down_ref[...].reshape(-1, 1024)
    for m in range(rows // tile):
        at = pl.ds(m * tile, tile)
        hidden = lax.dot_general(n_ref[at, :], up, NT, preferred_element_type=F32)
        hidden = gelu(hidden).astype(BF)
        acc_ref[at, :] += jnp.dot(hidden, down, preferred_element_type=F32)

    @pl.when(step == pl.num_programs(0) - 1)
    def _():
        out_ref[...] = acc_ref[...].astype(BF)


def tail(context, tokens, every, blocks=16):
    rows, width = context.shape
    flat = every.reshape(128, 96, width)
    whole = lambda i: (0, 0)
    return pl.pallas_call(
        tail_kernel,
        grid=(128 // blocks,),
        in_specs=[
            pl.BlockSpec((rows, width), whole),
            pl.BlockSpec((rows, width), whole),
            pl.BlockSpec(memory_space=pl.ANY),
            pl.BlockSpec((blocks, 32, width), lambda i: (i, 1, 0)),
            pl.BlockSpec((blocks, 32, width), lambda i: (i, 2, 0)),
        ],
        out_specs=pl.BlockSpec((rows, width), whole),
        out_shape=jax.ShapeDtypeStruct((rows, width), BF),
        scratch_shapes=[
            pltpu.VMEM((2, 4, 2, 2, 4, 8, width), BF),
            pltpu.VMEM((rows, width), BF),
            pltpu.VMEM((rows, width), F32),
            pltpu.SemaphoreType.DMA,
        ],
        compiler_params=pltpu.CompilerParams(
            dimension_semantics=("arbitrary",), vmem_limit_bytes=VMEM_LIMIT
        ),
        cost_estimate=pl.CostEstimate(
            flops=2 * rows * width * 9 * width,
            bytes_accessed=24 << 20,
            transcendentals=rows * 4096,
        ),
        name="tail",
    )(context, tokens, every, flat, flat)


AXES = ("zl", "y", "c", "zh", "x")
SIZES = (2, 4, 2, 2, 4)
LAT = ("zl", "y", "c")
LON = ("zh", "x")
TORUS = ("zh", "zl", "y", "x", "c")


def shifted(value, down, right):
    if right == 0:
        return lax.ppermute(value, LAT, [(i, (i + down) % 16) for i in range(16)])
    if down == 0:
        return lax.ppermute(value, LON, [(j, (j + right) % 8) for j in range(8)])
    pairs = [
        (i * 8 + j, (i + down) % 16 * 8 + (j + right) % 8) for i in range(16) for j in range(8)
    ]
    return lax.ppermute(value, AXES, pairs)


def layer_norm(values):
    widened = values.astype(F32)
    centre = jnp.mean(widened, axis=-1, keepdims=True)
    spread = jnp.mean(jnp.square(widened - centre), axis=-1, keepdims=True)
    return ((widened - centre) * lax.rsqrt(spread + 1e-05)).astype(BF)


def position_bias(bias_table):
    cell_ids = jnp.arange(64, dtype=jnp.int32)
    row_of, col_of = cell_ids // 8, cell_ids % 8
    offsets = (row_of[:, None] - row_of[None, :] + 7) * 15 + (col_of[:, None] - col_of[None, :] + 7)
    one_hot = (
        offsets.reshape(-1)[:, None] == jnp.arange(bias_table.shape[0], dtype=jnp.int32)[None, :]
    ).astype(F32)
    pos_bias = jnp.dot(one_hot, bias_table, precision=lax.Precision.HIGHEST)
    pos_bias = pos_bias.reshape(64, 64, bias_table.shape[1]).transpose(2, 0, 1)
    return jnp.tile(pos_bias, (1, 2, 2))


def window_mask(sea_mask, row_start, col_start):
    sea = lax.dynamic_slice(
        jnp.tile(sea_mask, (2, 2)), (row_start % 128, col_start % 256), (8, 32)
    )
    sea = sea.reshape(8, 4, 8).transpose(1, 0, 2).reshape(4, 64) == 1
    rows = (row_start + jnp.arange(8, dtype=jnp.int32)) % 128
    region = jnp.repeat(jnp.where(rows < 4, 2, jnp.where(rows >= 124, 1, 0)), 8)
    same_cell = jnp.eye(64, dtype=bool)
    allowed = (region[:, None] == region[None, :])[None] & (sea[:, None, :] | same_cell[None])
    allowed = allowed.reshape(2, 2, 64, 1, 64) & jnp.eye(2, dtype=bool)[None, :, None, :, None]
    return jnp.where(allowed, 0.0, -1e30).astype(F32).reshape(2, 128, 128)


def per_device(tokens, qkv_weight, proj_weight, up_weight, down_weight, bias_table, sea_mask):
    row_base = ((lax.axis_index("zl") * 4 + lax.axis_index("y")) * 2 + lax.axis_index("c")) * 8
    col_base = (lax.axis_index("zh") * 4 + lax.axis_index("x")) * 32
    shards = jnp.concatenate([qkv_weight, proj_weight, up_weight, down_weight], axis=0)
    every = lax.all_gather(shards, TORUS, axis=0, tiled=True).reshape(2, 2, 4, 4, 2, 96, 1024)
    bias = position_bias(bias_table)
    mask = window_mask(sea_mask, row_base + 4, col_base + 4)
    normed = layer_norm(tokens)
    low = shifted(normed[:, :4, 4:], -1, 0)
    right = shifted(normed[:, 4:, :4], 0, -1)
    corner = shifted(normed[:, :4, :4], -1, -1)
    feed = jnp.concatenate(
        [
            jnp.concatenate([normed[:, 4:, 4:], right], axis=2),
            jnp.concatenate([low, corner], axis=2),
        ],
        axis=1,
    )
    context = attention(feed.reshape(4, 8, 4, 8, 1024), every, bias, mask).reshape(4, 8, 32, 1024)
    up = shifted(context[:, 4:, :28], 1, 0)
    left = shifted(context[:, :4, 28:], 0, 1)
    corner = shifted(context[:, 4:, 28:], 1, 1)
    context = jnp.concatenate(
        [
            jnp.concatenate([corner, up], axis=2),
            jnp.concatenate([left, context[:, :4, :28]], axis=2),
        ],
        axis=1,
    )
    out = tail(context.reshape(-1, 1024), tokens.reshape(-1, 1024), every)
    return out.reshape(tokens.shape)


def solution(mesh):
    torus = Mesh(mesh.devices.reshape(SIZES), AXES)
    rows = P(LAT + LON, None)
    return jax.shard_map(
        per_device,
        mesh=torus,
        in_specs=(P(None, LAT, LON, None), rows, rows, rows, rows, P(), P()),
        out_specs=P(None, LAT, LON, None),
        check_vma=False,
    )
```

time: 271 us -> 205 us (0.76)
  local copies, waits for them, and re-layouts: 76.1 us -> 16.1 us
  matrix products: 61.5 us -> 2.58 us
  Pallas kernels: 0 us -> 56.1 us
  loops' own time: 4.81 us -> 0 us
  waiting for transfers between devices: 91.5 us -> 87.1 us
  starting transfers between devices: 12.3 us -> 15.6 us
    pallas_call x0 -> x2, Pallas kernels: none -> 56.1 us  [the longest x1 33.1 us: tail(): pl.pallas_call(tail_kernel, grid=(128 // blocks,), in_specs=[pl.BlockSpec...]
    dot_general x8 -> x1, matrix products: 46.3 us -> 2.58 us  [position_bias(): pos_bias = jnp.dot(one_hot, bias_table, precision=lax.Precision.HIGHEST)]
    transpose x8 -> x0, local copies, waits for them, and re-layouts: 41.3 us -> none  [the longest x7 35.8 us: gather_weights(): out.append(part.transpose(TO_LOGICAL + (5, 6)).reshape(-1, width))]
    sub x4 -> x0, matrix products: 15.2 us -> none  [one_group(): weights = jnp.exp(scores - row_top)]
    reshape x14 -> x1, local copies, waits for them, and re-layouts: 16 us -> 1.03 us  [position_bias(): pos_bias = pos_bias.reshape(64, 64, bias_table.shape[1]).transpose(2, 0, 1)]
    dynamic_slice x16 -> x0, local copies, waits for them, and re-layouts: 10.5 us -> none  [the longest x4 5.94 us: one_group(): lax.dynamic_slice_in_dim(pair_win, first_col, group_width, 3)]
    ppermute x4 -> x6, waiting for transfers between devices: 20.1 us -> 10.2 us  [the longest x2 6.91 us: shifted(): return lax.ppermute(value, AXES, pairs)]
    all_gather x1, waiting for transfers between devices: 71.3 us -> 76.9 us  [per_device(): lax.all_gather(shards, TORUS, axis=0, tiled=True)]
  transfers between devices with their start and end apart: 5 -> 7, of which waited for: 4 -> 3; matrix products, arithmetic and copies ran while one was open for 16% -> 11% of each run, Pallas kernels for 0% -> 0%
where the time goes in v2:
time: 205 us; the launch traced here: 203 us
  waiting for transfers between devices  87.1 us (42%)
  Pallas kernels  56.1 us (27%)
  local copies, waits for them, and re-layouts  16.1 us (8%)
  starting transfers between devices  15.6 us (8%)
  between operations  13.6 us (7%)
  other arithmetic  11.6 us (6%)
  matrix products  2.58 us (1%)
    all_gather x1, waiting for transfers between devices, per_device(): lax.all_gather(shards, TORUS, axis=0, tiled=True)  76.9 us
    pallas_call x1, Pallas kernels, tail(): pl.pallas_call(tail_kernel, grid=(128 // blocks,), in_specs=[pl.BlockSpec...  33.1 us
    pallas_call x1, Pallas kernels, attention(): pl.pallas_call(attention_kernel, grid=(batch // step,), in_specs=[pl.Bloc...  23 us
    ppermute x2, starting transfers between devices, shifted(): return lax.ppermute(value, LON, [(j, (j + right) % 8) for j in range(8)])  7.4 us
    ppermute x2, waiting for transfers between devices, shifted(): return lax.ppermute(value, AXES, pairs)  6.91 us
    ppermute x2, starting transfers between devices, shifted(): return lax.ppermute(value, AXES, pairs)  5.45 us
    another operation x2, local copies, waits for them, and re-layouts, position_bias(): return jnp.tile(pos_bias, (1, 2, 2))  4.15 us
  transfers between devices with their start and end apart: 7, of which 3 were waited for; matrix products, arithmetic and copies ran while one was open for 11% of the time, Pallas kernels for 0%

profile of v2, /device:TPU:1, one launch (start us, length us, event | category | flops | bytes accessed | tf_op | source)
XLA Modules:
  0.0 202.7 jit_solution(11985085042105304229)
XLA Ops:
  6.5 1.7 pad_maximum_fusion
  8.3 1.9 convert_reduce_fusion
  10.2 2.3 %fusion.2 = f32[4,8,32]{2,1,0:T(8,128)S(1)} fusion(bf16[4,8,32,1024]{3,2,1,0:T(8,128)(2,1)} %param.7, f32[4,8,32]{2,1,0:T(8,128)S(1)} %broadcast_multiply_fusion), kind=kLoop, calls=%fused_computation.4 | loop fusion | flops 4193280 | bytes 2105344 | tf_op jit(solution)/shard_map/reduce_sum | solution.py:218
  13.1 2.0 %fusion.9 = (bf16[4,4,28,1024]{3,2,1,0:T(8,128)(2,1)S(1)}, bf16[4,4,28,1024]{3,2,1,0:T(8,128)(2,1)}) fusion(bf16[4,8,32,1024]{3,2,1,0:T(8,128)(2,1)S(1)} %fusion.3), kind=kLoop, calls=%fused_computation.34 | loop fusion | bytes 3670016 | tf_op jit(solution)/shard_map/slice | solution.py:260
  15.2 1.4 collective-permute-start.1
  17.3 5.9 %collective-permute-start = (bf16[4,4,4,1024]{3,2,1,0:T(4,128)(2,1)}, bf16[4,4,4,1024]{3,2,1,0:T(4,128)(2,1)S(1)}, u32[]{:S(2)}, u32[]{:S(2)}) collective-permute-start(bf16[4,4,4,1024]{3,2,1,0:T(4,128)(2,1)} %get-tuple-element.11), channel_id=1, source_target_pairs={{0,7},{1,0},{2,1},{3,2},{4,3},{5,4},{6,5},{7,6},{8,15},{9,8},{10,9... | collective-permute-start | bytes 393224 | tf_op jit(solution)/shard_map/ppermute | solution.py:208
  23.2 4.2 %collective-permute-start.2 = (bf16[4,4,4,1024]{3,2,1,0:T(4,128)(2,1)}, bf16[4,4,4,1024]{3,2,1,0:T(4,128)(2,1)S(1)}, u32[]{:S(2)}, u32[]{:S(2)}) collective-permute-start(bf16[4,4,4,1024]{3,2,1,0:T(4,128)(2,1)} %get-tuple-element.12), channel_id=1, source_target_pairs={{0,127},{1,120},{2,121},{3,122},{4,123},{5,124},{6,125},{7,126},{8... | collective-permute-start | bytes 393224 | tf_op jit(solution)/shard_map/ppermute | solution.py:212
  28.9 2.6 %fusion.4 = f32[4096,16]{0,1:T(8,128)S(1)} fusion(f32[225,16]{0,1:T(8,128)S(1)} %copy-done, s32[4096]{0:T(1024)S(1)} %add.106), kind=kOutput, calls=%fused_computation.7 | convolution fusion | flops 177868800 | bytes 292928 | tf_op jit(solution)/shard_map/dot_general | solution.py:229
  31.5 1.0 reshape.189
  32.5 2.0 tile.8
  34.5 2.2 %tile.9.bias_ref = f32[16,128,128]{2,1,0:T(8,128)} reshape(f32[16,2,64,2,64]{4,3,2,1,0:T(2,128)S(1)} %tile.8) | data formatting | bytes 2097152 | tf_op jit(solution)/shard_map/tile | solution.py:231
  37.3 3.0 %maximum_bitcast_fusion.x_ref = bf16[4,8,4,8,1024]{4,3,2,1,0:T(8,128)(2,1)} fusion(bf16[4,4,4,1024]{3,2,1,0:T(4,128)(2,1)S(1)} %collective-permute-done.2, bf16[4,4,28,1024]{3,2,1,0:T(8,128)(2,1)} %collective-permute-done.1, bf16[4,4,4,1024]{3,2,1,0:T(4,128)(2,1)S(1)} %collective-permute-done, bf16[4,4,28,1024]{3,2,1,0:T(8,128)(2,1)S(1)} %get-tuple-element.9), kind=kLoop, calls=%fused_computation.8 | loop fusion | flops 8388608 | bytes 4194304 | tf_op jit(solution)/shard_map/reshape | solution.py:265
  40.4 76.9 %all-gather.2.cloned.1.call-done = bf16[12288,1024]{1,0:T(8,128)(2,1)} async-done(((bf16[96,1024]{1,0:T(8,128)(2,1)}), bf16[12288,1024]{1,0:T(8,128)(2,1)}) %all-gather.2.cloned.1.call-update) | async-done | bytes 25165840 | tf_op jit(solution)/shard_map/all_gather | solution.py:251
  117.3 23.0 %attention.1 = bf16[4,8,4,8,1024]{4,3,2,1,0:T(8,128)(2,1)} custom-call(bf16[4,8,4,8,1024]{4,3,2,1,0:T(8,128)(2,1)} %maximum_bitcast_fusion.x_ref, bf16[2,2,4,4,2,96,1024]{6,5,4,3,2,1,0:T(8,128)(2,1)} %bitcast.16, f32[16,128,128]{2,1,0:T(8,128)} %tile.9.bias_ref, f32[2,128,128]{2,1,0:T(8,128)} %and_select_fusion.mask_ref), custom_call_target="tpu_custom_call" | custom-call | flops 6442450944 | bytes 12582912 | tf_op jit(solution)/shard_map/attention/pallas_call | solution.py:88
  140.3 1.7 fusion.8
  142.8 1.4 collective-permute-start.4
  144.1 1.2 fusion.7
  145.4 1.2 collective-permute-start.3
  146.7 1.5 collective-permute-start.5
  148.9 6.9 %collective-permute-done.3 = bf16[4,4,4,1024]{3,1,2,0:T(4,128)(2,1)S(1)} collective-permute-done((bf16[4,4,4,1024]{3,1,2,0:T(4,128)(2,1)S(1)}, bf16[4,4,4,1024]{3,1,2,0:T(4,128)(2,1)S(1)}, u32[]{:S(2)}, u32[]{:S(2)}) %collective-permute-start.3) | collective-permute-done | bytes 131104 | tf_op jit(solution)/shard_map/ppermute | solution.py:212
  155.8 3.3 %collective-permute-done.5 = bf16[4,4,4,1024]{3,1,2,0:T(4,128)(2,1)S(1)} collective-permute-done((bf16[4,4,4,1024]{3,1,2,0:T(4,128)(2,1)S(1)}, bf16[4,4,4,1024]{3,1,2,0:T(4,128)(2,1)S(1)}, u32[]{:S(2)}, u32[]{:S(2)}) %collective-permute-start.5) | collective-permute-done | bytes 131104 | tf_op jit(solution)/shard_map/ppermute | solution.py:208
  159.1 1.1 maximum_maximum_fusion
  160.2 2.5 %copy.14 = bf16[4,8,32,1024]{3,2,1,0:T(8,128)(2,1)} copy(bf16[4,8,32,1024]{3,1,2,0:T(8,128)(2,1)S(1)} %maximum_maximum_fusion) | data formatting | bytes 4194304 | tf_op jit(solution)/shard_map/concatenate | solution.py:269
  162.7 33.1 %tail.1 = bf16[1024,1024]{1,0:T(8,128)(2,1)} custom-call(bf16[1024,1024]{1,0:T(8,128)(2,1)} %bitcast.23, bf16[1024,1024]{1,0:T(8,128)(2,1)} %bitcast.20, bf16[2,2,4,4,2,96,1024]{6,5,4,3,2,1,0:T(8,128)(2,1)} %bitcast.17, bf16[128,96,1024]{2,1,0:T(8,128)(2,1)} %bitcast.18, bf16[128,96,1024]{2,1,0:T(8,128)(2,1)} %bitcast.19), custom_call_target="tpu_custom_call" | custom-call | flops 19327352832 | bytes 25165824 | tf_op jit(solution)/shard_map/tail/pallas_call | solution.py:167
  (40 shorter events, 5.0 us)
Async XLA Ops:
  6.5 22.4 %copy-start = (f32[225,16]{0,1:T(8,128)S(1)}, f32[225,16]{0,1:T(8,128)}, u32[]{:S(2)}) copy-start(f32[225,16]{0,1:T(8,128)} %param.12) | copy-start | bytes 43204
  6.5 6.0 %copy-start.1 = (bf16[4,8,32,1024]{3,2,1,0:T(8,128)(2,1)S(1)}, bf16[4,8,32,1024]{3,2,1,0:T(8,128)(2,1)}, u32[]{:S(2)}) copy-start(bf16[4,8,32,1024]{3,2,1,0:T(8,128)(2,1)} %param.7) | copy-start | bytes 6291460
  6.5 110.7 %all-gather.2.cloned.1.call-start = ((), (), s32[]{:S(2)}) async-start(), calls=%async_computation | async-start | bytes 25362432 | tf_op jit(solution)/shard_map/all_gather | solution.py:251
  12.5 14.9 %copy-start.2 = (s32[128,256]{1,0:T(8,128)S(1)}, s32[128,256]{1,0:T(8,128)}, u32[]{:S(2)}) copy-start(s32[128,256]{1,0:T(8,128)} %param.13) | copy-start | bytes 393220
  15.2 22.2 %collective-permute-start.1 = (bf16[4,4,28,1024]{3,2,1,0:T(8,128)(2,1)}, bf16[4,4,28,1024]{3,2,1,0:T(8,128)(2,1)}, u32[]{:S(2)}, u32[]{:S(2)}) collective-permute-start(bf16[4,4,28,1024]{3,2,1,0:T(8,128)(2,1)} %get-tuple-element.10), channel_id=1, source_target_pairs={{0,120},{8,0},{16,8},{24,16},{32,24},{40,32},{48,40},{56,48},{64,5... | collective-permute-start | bytes 2752520 | tf_op jit(solution)/shard_map/ppermute | solution.py:206
  17.3 20.0 %collective-permute-start = (bf16[4,4,4,1024]{3,2,1,0:T(4,128)(2,1)}, bf16[4,4,4,1024]{3,2,1,0:T(4,128)(2,1)S(1)}, u32[]{:S(2)}, u32[]{:S(2)}) collective-permute-start(bf16[4,4,4,1024]{3,2,1,0:T(4,128)(2,1)} %get-tuple-element.11), channel_id=1, source_target_pairs={{0,7},{1,0},{2,1},{3,2},{4,3},{5,4},{6,5},{7,6},{8,15},{9,8},{10,9... | collective-permute-start | bytes 393224 | tf_op jit(solution)/shard_map/ppermute | solution.py:208
  23.2 14.1 %collective-permute-start.2 = (bf16[4,4,4,1024]{3,2,1,0:T(4,128)(2,1)}, bf16[4,4,4,1024]{3,2,1,0:T(4,128)(2,1)S(1)}, u32[]{:S(2)}, u32[]{:S(2)}) collective-permute-start(bf16[4,4,4,1024]{3,2,1,0:T(4,128)(2,1)} %get-tuple-element.12), channel_id=1, source_target_pairs={{0,127},{1,120},{2,121},{3,122},{4,123},{5,124},{6,125},{7,126},{8... | collective-permute-start | bytes 393224 | tf_op jit(solution)/shard_map/ppermute | solution.py:212
  142.8 16.4 %collective-permute-start.4 = (bf16[4,4,28,1024]{3,1,2,0:T(4,128)(2,1)S(1)}, bf16[4,4,28,1024]{3,1,2,0:T(4,128)(2,1)S(1)}, u32[]{:S(2)}, u32[]{:S(2)}) collective-permute-start(bf16[4,4,28,1024]{3,1,2,0:T(4,128)(2,1)S(1)} %copy.16), channel_id=1, source_target_pairs={{0,8},{8,16},{16,24},{24,32},{32,40},{40,48},{48,56},{56,64},{64,7... | collective-permute-start | bytes 2752520 | tf_op jit(solution)/shard_map/ppermute | solution.py:206
  145.4 10.4 %collective-permute-start.3 = (bf16[4,4,4,1024]{3,1,2,0:T(4,128)(2,1)S(1)}, bf16[4,4,4,1024]{3,1,2,0:T(4,128)(2,1)S(1)}, u32[]{:S(2)}, u32[]{:S(2)}) collective-permute-start(bf16[4,4,4,1024]{3,1,2,0:T(4,128)(2,1)S(1)} %copy.15), channel_id=1, source_target_pairs={{0,9},{1,10},{2,11},{3,12},{4,13},{5,14},{6,15},{7,8},{8,17},{9,18... | collective-permute-start | bytes 393224 | tf_op jit(solution)/shard_map/ppermute | solution.py:212
  146.7 12.4 %collective-permute-start.5 = (bf16[4,4,4,1024]{3,1,2,0:T(4,128)(2,1)S(1)}, bf16[4,4,4,1024]{3,1,2,0:T(4,128)(2,1)S(1)}, u32[]{:S(2)}, u32[]{:S(2)}) collective-permute-start(bf16[4,4,4,1024]{3,1,2,0:T(4,128)(2,1)S(1)} %copy.17), channel_id=1, source_target_pairs={{0,1},{1,2},{2,3},{3,4},{4,5},{5,6},{6,7},{7,0},{8,9},{9,10},{10,1... | collective-permute-start | bytes 393224 | tf_op jit(solution)/shard_map/ppermute | solution.py:208
Sparse Core Ops, SparseCore 0:
  10.4 106.7 all-gather.1
